TPU v7x, 32 devices: a whole 2x2x4 slice. The times are simulated.
32 devices in a mesh: row: 8 (over z, y), col: 4 (over x, core).
Axes of the slice: x: 2, y: 2, z: 4, core: 2. Of those that a mesh axis runs over, the one named last changes fastest.
Arguments:
- noise: float32 [8192, 512], P(('row', 'col')), may hold values from -40 to 40
- data: float32 [8192, 512], P(('col', 'row')), may hold values from -6 to 6
Outputs:
- noise_target: float32 [8192, 512], P(('row', 'col'))
- data_target: float32 [8192, 512], P(('col', 'row'))
- f_potential: float32 [8192], P('row')
- g_potential: float32 [8192], P('col')
All inputs are finite; a program needn't handle non-finite values.
Results may differ from a plain program's by a relative error of at most 0.0003.
Values sent between devices are 32-bit elements; how exact they have to be, the bound alone decides.
A program may use at most 64 MiB of HBM per device.

v0:
```python
import jax
import jax.numpy as jnp
from jax import lax
from jax.sharding import PartitionSpec as P

ITERS = 2


EPSILON = 32.0


def row_stats(scores):
    peak = lax.pmax(jnp.max(scores, axis=1), "col")
    total = lax.psum(jnp.sum(jnp.exp(scores - peak[:, None]), axis=1), "col")
    return (peak, total)


def col_stats(scores):
    peak = lax.pmax(jnp.max(scores, axis=0), "row")
    total = lax.psum(jnp.sum(jnp.exp(scores - peak[None, :]), axis=0), "row")
    return (peak, total)


def shards(noise, data):
    x_full = lax.all_gather(noise, "col", axis=0, tiled=True)
    y_full = lax.all_gather(data, "row", axis=0, tiled=True)
    x_norm = jnp.sum(x_full * x_full, axis=1)
    y_norm = jnp.sum(y_full * y_full, axis=1)
    inner = jnp.dot(
        x_full, y_full.T, precision=lax.Precision.HIGHEST, preferred_element_type=jnp.float32
    )
    cost = x_norm[:, None] + y_norm[None, :] - 2.0 * inner
    g_now = jnp.zeros((cost.shape[1],), jnp.float32)
    f_now = jnp.zeros((cost.shape[0],), jnp.float32)
    col_scores = cost
    col_peak = g_now
    col_total = g_now
    for step in range(ITERS):
        row_scores = (g_now[None, :] - cost) / EPSILON
        peak, total = row_stats(row_scores)
        f_now = -EPSILON * (peak + jnp.log(total))
        col_scores = (f_now[:, None] - cost) / EPSILON
        col_peak, col_total = col_stats(col_scores)
        g_now = -EPSILON * (col_peak + jnp.log(col_total))
    col_weights = jnp.exp(col_scores - col_peak[None, :]) / col_total[None, :]
    data_part = jnp.dot(
        col_weights.T, x_full, precision=lax.Precision.HIGHEST, preferred_element_type=jnp.float32
    )
    data_target = lax.psum_scatter(data_part, "row", scatter_dimension=0, tiled=True)
    final_scores = (g_now[None, :] - cost) / EPSILON
    peak, total = row_stats(final_scores)
    weights = jnp.exp(final_scores - peak[:, None]) / total[:, None]
    noise_part = jnp.dot(
        weights, y_full, precision=lax.Precision.HIGHEST, preferred_element_type=jnp.float32
    )
    noise_target = lax.psum_scatter(noise_part, "col", scatter_dimension=0, tiled=True)
    return (noise_target, data_target, f_now, g_now)


def solution(mesh):
    placed = (P(("row", "col"), None), P(("col", "row"), None))
    return jax.shard_map(
        shards,
        mesh=mesh,
        in_specs=placed,
        out_specs=(P(("row", "col"), None), P(("col", "row"), None), P("row"), P("col")),
        check_vma=False,
    )
```

profile of v0, /device:TPU:0, one launch (start us, length us, event | category | flops | bytes accessed | tf_op | source)
XLA Modules:
  0.0 431.4 jit_solution(6373098548882051552)
XLA Ops:
  7.2 0.0 all-gather.3.cloned.1.call-start
  7.2 0.7 all-gather.3.cloned.1.call-update
  7.9 0.0 all-gather.5.cloned.1.call-start
  7.9 0.7 all-gather.5.cloned.1.call-update
  8.6 0.0 reduce-scatter.3.cloned.1.call-start
  8.7 26.2 %all-gather.3.cloned.1.call-done = f32[1024,512]{1,0:T(8,128)} async-done(((f32[256,512]{1,0:T(8,128)}), f32[1024,512]{1,0:T(8,128)}) %all-gather.3.cloned.1.call-update) | async-done | bytes 2097168 | tf_op jit(solution)/shard_map/all_gather | solution.py:25
  34.8 1.8 multiply_reduce_fusion.1
  36.7 73.1 %all-gather.5.cloned.1.call-done = f32[2048,512]{1,0:T(8,128)} async-done(((f32[256,512]{1,0:T(8,128)}), f32[2048,512]{1,0:T(8,128)}) %all-gather.5.cloned.1.call-update) | async-done | bytes 4194320 | tf_op jit(solution)/shard_map/all_gather | solution.py:26
  109.8 2.5 multiply_reduce_fusion
  112.3 18.8 %fusion.4 = (f32[1024]{0:T(1024)S(1)}, f32[1024,2048]{1,0:T(8,128)}) fusion(f32[1024,512]{1,0:T(8,128)} %all-gather.3.cloned.1.call-done, f32[2048,512]{1,0:T(8,128)} %all-gather.5.cloned.1.call-done, f32[2048]{0:T(1024)S(1)} %multiply_reduce_fusion, f32[1024]{0:T(1024)S(1)} %multiply_reduce_fusion.1), kind=kOutput, calls=%fused_computation.15 | convolution fusion | flops 12897483776 | bytes 14696448 | tf_op jit(solution)/shard_map/dot_general | solution.py:29
  131.1 5.6 %pmax.35 = f32[1024]{0:T(1024)S(1)} all-reduce(f32[1024]{0:T(1024)S(1)} %get-tuple-element.4), channel_id=1, replica_groups=mesh['row'=8,'col'=4] {'col'}, use_global_device_ids=true, to_apply=%region_3.0 | all-reduce | flops 1024 | bytes 8192 | tf_op jit(solution)/shard_map/pmax | solution.py:13
  136.7 4.5 %exponential_reduce_fusion.2 = f32[1024]{0:T(1024)S(1)} fusion(f32[1024,2048]{1,0:T(8,128)} %get-tuple-element.5, f32[1024]{0:T(1024)S(1)} %pmax.35), kind=kLoop, calls=%fused_computation.12 | loop fusion | flops 8387584 | bytes 8396800 | tf_op jit(solution)/shard_map/reduce_sum | solution.py:14
  141.2 6.6 %psum.35 = f32[1024]{0:T(1024)S(1)} all-reduce(f32[1024]{0:T(1024)S(1)} %exponential_reduce_fusion.2), channel_id=1, replica_groups=mesh['row'=8,'col'=4] {'col'}, use_global_device_ids=true, to_apply=%region_5.0 | all-reduce | flops 1024 | bytes 8192 | tf_op jit(solution)/shard_map/psum | solution.py:14
  147.8 4.3 fusion.5
  152.1 19.2 %pmax.36 = f32[2048]{0:T(1024)S(1)} all-reduce(f32[2048]{0:T(1024)S(1)} %fusion.5), channel_id=1, replica_groups=mesh['row'=8,'col'=4] {'row'}, use_global_device_ids=true, to_apply=%region_7.0 | all-reduce | flops 2048 | bytes 16384 | tf_op jit(solution)/shard_map/pmax | solution.py:19
  171.4 4.5 %exponential_reduce_fusion.1 = f32[2048]{0:T(1024)S(1)} fusion(f32[1024,2048]{1,0:T(8,128)} %get-tuple-element.5, f32[2048]{0:T(1024)S(1)} %pmax.36, f32[1024]{0:T(1024)S(1)} %add_multiply_fusion.3), kind=kLoop, calls=%fused_computation.10 | loop fusion | flops 8386560 | bytes 8409088 | tf_op jit(solution)/shard_map/reduce_sum | solution.py:20
  175.9 17.7 %psum.36 = f32[2048]{0:T(1024)S(1)} all-reduce(f32[2048]{0:T(1024)S(1)} %exponential_reduce_fusion.1), channel_id=1, replica_groups=mesh['row'=8,'col'=4] {'row'}, use_global_device_ids=true, to_apply=%region_9.0 | all-reduce | flops 2048 | bytes 16384 | tf_op jit(solution)/shard_map/psum | solution.py:20
  193.6 4.3 fusion.6
  197.9 5.7 %pmax.37 = f32[1024]{0:T(1024)S(1)} all-reduce(f32[1024]{0:T(1024)S(1)} %fusion.6), channel_id=1, replica_groups=mesh['row'=8,'col'=4] {'col'}, use_global_device_ids=true, to_apply=%region_11.0 | all-reduce | flops 1024 | bytes 8192 | tf_op jit(solution)/shard_map/pmax | solution.py:13
  203.6 4.5 %exponential_reduce_fusion = f32[1024]{0:T(1024)S(1)} fusion(f32[1024,2048]{1,0:T(8,128)} %get-tuple-element.5, f32[1024]{0:T(1024)S(1)} %pmax.37, f32[2048]{0:T(1024)S(1)} %add_multiply_fusion.1), kind=kLoop, calls=%fused_computation.8 | loop fusion | flops 8387584 | bytes 8404992 | tf_op jit(solution)/shard_map/reduce_sum | solution.py:14
  208.1 6.3 %psum.37 = f32[1024]{0:T(1024)S(1)} all-reduce(f32[1024]{0:T(1024)S(1)} %exponential_reduce_fusion), channel_id=1, replica_groups=mesh['row'=8,'col'=4] {'col'}, use_global_device_ids=true, to_apply=%region_13.0 | all-reduce | flops 1024 | bytes 8192 | tf_op jit(solution)/shard_map/psum | solution.py:14
  214.4 0.0 copy-start.2
  214.4 4.3 fusion.7
  218.6 19.1 %pmax.38 = f32[2048]{0:T(1024)S(1)} all-reduce(f32[2048]{0:T(1024)S(1)} %fusion.7), channel_id=1, replica_groups=mesh['row'=8,'col'=4] {'row'}, use_global_device_ids=true, to_apply=%region_15.0 | all-reduce | flops 2048 | bytes 16384 | tf_op jit(solution)/shard_map/pmax | solution.py:19
  237.8 4.5 %fusion.9 = f32[2048]{0:T(1024)S(1)} fusion(f32[1024,2048]{1,0:T(8,128)} %get-tuple-element.5, f32[2048]{0:T(1024)S(1)} %pmax.38, f32[1024]{0:T(1024)S(1)} %add_multiply_fusion.2), kind=kLoop, calls=%fused_computation.20 | loop fusion | flops 8386560 | bytes 8409088 | tf_op jit(solution)/shard_map/reduce_sum | solution.py:20
  242.3 17.7 %psum.38 = f32[2048]{0:T(1024)S(1)} all-reduce(f32[2048]{0:T(1024)S(1)} %fusion.9), channel_id=1, replica_groups=mesh['row'=8,'col'=4] {'row'}, use_global_device_ids=true, to_apply=%region_17.0 | all-reduce | flops 2048 | bytes 16384 | tf_op jit(solution)/shard_map/psum | solution.py:20
  260.0 0.0 copy-start.1
  260.0 4.3 fusion.8
  264.3 5.7 %pmax.39 = f32[1024]{0:T(1024)S(1)} all-reduce(f32[1024]{0:T(1024)S(1)} %fusion.8), channel_id=1, replica_groups=mesh['row'=8,'col'=4] {'col'}, use_global_device_ids=true, to_apply=%region_19.0 | all-reduce | flops 1024 | bytes 8192 | tf_op jit(solution)/shard_map/pmax | solution.py:13
  270.0 4.5 %fusion.10 = f32[1024]{0:T(1024)S(1)} fusion(f32[1024,2048]{1,0:T(8,128)} %get-tuple-element.5, f32[1024]{0:T(1024)S(1)} %pmax.39, f32[2048]{0:T(1024)S(1)} %add_multiply_fusion), kind=kLoop, calls=%fused_computation.21 | loop fusion | flops 8387584 | bytes 8404992 | tf_op jit(solution)/shard_map/reduce_sum | solution.py:14
  274.4 6.5 %psum.39 = f32[1024]{0:T(1024)S(1)} all-reduce(f32[1024]{0:T(1024)S(1)} %fusion.10), channel_id=1, replica_groups=mesh['row'=8,'col'=4] {'col'}, use_global_device_ids=true, to_apply=%region_21.0 | all-reduce | flops 1024 | bytes 8192 | tf_op jit(solution)/shard_map/psum | solution.py:14
  281.0 0.0 copy-done.1
  281.0 0.0 copy-start
  281.0 22.4 %fusion.2 = f32[1024,512]{1,0:T(8,128)} fusion(f32[2048,512]{1,0:T(8,128)} %all-gather.5.cloned.1.call-done, f32[1024,2048]{1,0:T(8,128)} %get-tuple-element.5, f32[1024]{0:T(1024)S(1)} %psum.39, f32[1024]{0:T(1024)S(1)} %pmax.39, f32[2048]{0:T(1024)S(1)} %add_multiply_fusion), kind=kOutput, calls=%fused_computation.2 | convolution fusion | flops 12893290496 | bytes 14696448 | tf_op jit(solution)/shard_map/dot_general | solution.py:53
  303.4 0.0 reduce-scatter.3.cloned.1.call-update
  303.4 0.3 reduce-scatter.5.cloned.1.call-start
  303.7 0.0 copy-done.2
  303.7 0.0 copy-done
  303.7 18.5 %fusion = f32[2048,512]{1,0:T(8,128)} fusion(f32[1024,512]{1,0:T(8,128)S(1)} %copy-done, f32[1024,2048]{1,0:T(8,128)} %get-tuple-element.5, f32[2048]{0:T(1024)S(1)} %psum.38, f32[2048]{0:T(1024)S(1)} %pmax.38, f32[1024]{0:T(1024)S(1)} %add_multiply_fusion.2), kind=kOutput, calls=%fused_computation | convolution fusion | flops 12893290496 | bytes 14700544 | tf_op jit(solution)/shard_map/dot_general | solution.py:46
  322.2 0.0 reduce-scatter.5.cloned.1.call-update
  322.3 10.3 %reduce-scatter.3.cloned.1.call-done = f32[256,512]{1,0:T(8,128)} async-done(((f32[1024,512]{1,0:T(8,128)}), f32[256,512]{1,0:T(8,128)}) %reduce-scatter.3.cloned.1.call-update) | async-done | bytes 524304 | tf_op jit(solution)/shard_map/reduce_scatter | solution.py:56
  332.5 92.4 %reduce-scatter.5.cloned.1.call-done = f32[256,512]{1,0:T(8,128)} async-done(((f32[2048,512]{1,0:T(8,128)}), f32[256,512]{1,0:T(8,128)}) %reduce-scatter.5.cloned.1.call-update) | async-done | bytes 524304 | tf_op jit(solution)/shard_map/reduce_scatter | solution.py:49
  (4 shorter events, 0.0 us)
Async XLA Ops:
  7.2 27.7 %all-gather.3.cloned.1.call-start = ((), (), s32[]{:S(2)}) async-start(), calls=%async_computation.2 | async-start | bytes 2621440 | tf_op jit(solution)/shard_map/all_gather | solution.py:25
  7.9 101.9 %all-gather.5.cloned.1.call-start = ((), (), s32[]{:S(2)}) async-start(), calls=%async_computation.3 | async-start | bytes 4718592 | tf_op jit(solution)/shard_map/all_gather | solution.py:26
  8.6 323.9 %reduce-scatter.3.cloned.1.call-start = ((), (), s32[]{:S(2)}) async-start(), calls=%async_computation.4 | async-start | bytes 2621440 | tf_op jit(solution)/shard_map/reduce_scatter | solution.py:56
  214.4 89.3 %copy-start.2 = (f32[1024]{0:T(1024)}, f32[1024]{0:T(1024)S(1)}, u32[]{:S(2)}) copy-start(f32[1024]{0:T(1024)S(1)} %add_multiply_fusion.2) | copy-start | bytes 12292
  260.0 21.0 %copy-start.1 = (f32[2048]{0:T(1024)}, f32[2048]{0:T(1024)S(1)}, u32[]{:S(2)}) copy-start(f32[2048]{0:T(1024)S(1)} %add_multiply_fusion) | copy-start | bytes 24580
  281.0 22.7 %copy-start = (f32[1024,512]{1,0:T(8,128)S(1)}, f32[1024,512]{1,0:T(8,128)}, u32[]{:S(2)}) copy-start(f32[1024,512]{1,0:T(8,128)} %all-gather.3.cloned.1.call-done) | copy-start | bytes 6291460
  303.4 121.5 %reduce-scatter.5.cloned.1.call-start = ((), (), s32[]{:S(2)}) async-start(), calls=%async_computation.5 | async-start | bytes 4718592 | tf_op jit(solution)/shard_map/reduce_scatter | solution.py:49
Sparse Core Ops, SparseCore 0:
  9.5 25.2 all-gather.2
  37.0 72.7 all-gather.4
  303.5 28.9 reduce-scatter.2
  336.6 88.2 reduce-scatter.4
where the time goes:
time: 432 us; the launch traced here: 431 us
  waiting for transfers between devices  203 us (47%)
  blocking collectives  110 us (25%)
  matrix products  59.7 us (14%)
  other arithmetic  43.9 us (10%)
  between operations  13.9 us (3%)
    reduce_scatter x1, waiting for transfers between devices, shards(): lax.psum_scatter(data_part, 'row', scatter_dimension=0, tiled=True)  92.4 us
    all_gather x1, waiting for transfers between devices, shards(): y_full = lax.all_gather(data, 'row', axis=0, tiled=True)  73.1 us
    pmax x2, blocking collectives, col_stats(): peak = lax.pmax(jnp.max(scores, axis=0), 'row')  38.4 us
    psum x2, blocking collectives, col_stats(): total = lax.psum(jnp.sum(jnp.exp(scores - peak[None, :]), axis=0), 'row')  35.4 us
    all_gather x1, waiting for transfers between devices, shards(): x_full = lax.all_gather(noise, 'col', axis=0, tiled=True)  26.2 us
    dot_general x1, matrix products, shards(): jnp.dot(weights, y_full, precision=lax.Precision.HIGHEST, preferred_eleme...  22.4 us
    psum x3, blocking collectives, row_stats(): total = lax.psum(jnp.sum(jnp.exp(scores - peak[:, None]), axis=1), 'col')  19.4 us
    dot_general x1, matrix products, shards(): jnp.dot(x_full, y_full.T, precision=lax.Precision.HIGHEST, preferred_elem...  18.8 us
  transfers between devices with their start and end apart: 4, of which 4 were waited for; matrix products, arithmetic and copies ran while one was open for 5% of the time, Pallas kernels for 0%

commit v1 on v0

v1 whole, which is shorter than its diff:
```python
import functools
import math

import jax
import jax.numpy as jnp
from jax import lax
from jax.experimental import pallas as pl
from jax.experimental.pallas import tpu as pltpu
from jax.sharding import PartitionSpec as P

MESH = pl.DeviceIdType.MESH
EPSILON = 32.0
UNIT = math.log2(math.e) / EPSILON
BACK = EPSILON * math.log(2.0)
SCALE = 2.0 * UNIT


def split(v):
    hi = v.astype(jnp.bfloat16)
    return hi, (v - hi.astype(jnp.float32)).astype(jnp.bfloat16)


def dot3(ah, al, bh, bl):
    d = functools.partial(jnp.dot, preferred_element_type=jnp.float32)
    return d(ah, bh) + (d(ah, bl) + d(al, bh))


def kernel(
    nr, nc,
    x_ref, y_ref,
    nt_ref, dt_ref, f_ref, g_ref,
    x_full, y_full, scores, xsh, xsl, xth, xtl, ysh, ysl, yth, ytl,
    eh, el, part, npart, pm, ps, fcol, xn, yn, gvec, cloc,
    rstat, cstat, rsbuf, first, nsbuf,
    ag_s, ag_r, x_s, x_r, rst_s, rst_r, cst_s, cst_r, rs_s, rs_r, ns_s, ns_r,
):
    row, col = lax.axis_index("row"), lax.axis_index("col")
    xb, w = x_ref.shape
    yb = y_ref.shape[0]
    rows, cols = scores.shape
    half, hw = yb // 2, w // 2

    def index_of(p):
        q = lax.div(p, nr // 2)
        return (1 - q) * (2 * p) + q * (2 * (nr - 1 - p) + 1)

    odd = lax.rem(row, 2)
    pos = (1 - odd) * lax.div(row, 2) + odd * (nr - 1 - lax.div(row, 2))

    def at(d):
        return index_of(lax.rem(pos + d + 2 * nr, nr))

    sides = (1, -1)
    barrier = pltpu.get_barrier_semaphore()
    for o in range(1, nr):
        pl.semaphore_signal(barrier, inc=1, device_id=(lax.rem(row + o, nr), col), device_id_type=MESH)
    for o in range(1, nc):
        pl.semaphore_signal(barrier, inc=1, device_id=(row, lax.rem(col + o, nc)), device_id_type=MESH)
    pl.semaphore_wait(barrier, nr + nc - 2)

    pending = []

    def send(src, dst, ss, rs, dev):
        c = pltpu.make_async_remote_copy(src_ref=src, dst_ref=dst, send_sem=ss, recv_sem=rs, device_id=dev, device_id_type=MESH)
        c.start()
        pending.append(c)

    def arrive(dst, ss, rs, dev):
        pltpu.make_async_remote_copy(src_ref=dst, dst_ref=dst, send_sem=ss, recv_sem=rs, device_id=dev, device_id_type=MESH).wait_recv()

    def piece(ref, o, d):
        return ref.at[o, pl.ds(d * half, half)]

    def ag_send(s):
        for d in range(2):
            o = at(-sides[d] * s)
            src = y_ref.at[pl.ds(d * half, half)] if s == 0 else piece(y_full, o, d)
            send(src, piece(y_full, o, d), ag_s.at[s, d], ag_r.at[s, d], (at(sides[d]), col))

    def ag_wait(s):
        for d in range(2):
            o = at(-sides[d] * (s + 1))
            arrive(piece(y_full, o, d), ag_s.at[s, d], ag_r.at[s, d], (at(sides[d]), col))

    def peers(n, me, ss, rs, src, dst, dev):
        for o in range(1, n):
            send(src, dst, ss.at[o], rs.at[me], dev(lax.rem(me + o, n)))

    def peers_wait(n, me, ss, rs, dst, dev):
        for o in range(1, n):
            k = lax.rem(me + o, n)
            arrive(dst(k), ss.at[o], rs.at[k], dev(k))

    in_col = lambda k: (row, k)
    in_row = lambda k: (k, col)

    ag_send(0)
    peers(nc, col, x_s, x_r, x_ref, x_full.at[col], in_col)
    x_full[col] = x_ref[...]
    y_full[row] = y_ref[...]

    def prep_x(k, _):
        r0 = pl.ds(pl.multiple_of(k * xb, xb), xb)
        v = x_full[k] * SCALE
        xsh[r0, :], xsl[r0, :] = split(v)
        t = v.T
        xth[:, r0], xtl[:, r0] = split(t)
        xn[:, r0] = jnp.sum(t * t, axis=0, keepdims=True) * (1.0 / (SCALE * SCALE))
        return 0

    tile = 256

    def block(o):
        c0 = pl.ds(pl.multiple_of(o * yb, yb), yb)
        v = y_full[o]
        ysh[c0, :], ysl[c0, :] = split(v)
        t = v.T
        yth[...], ytl[...] = split(t)
        yn[:, c0] = jnp.sum(t * t, axis=0, keepdims=True)

        def body(i, _):
            r0 = pl.ds(pl.multiple_of(i * tile, tile), tile)
            scores[r0, c0] = dot3(xsh[r0, :], xsl[r0, :], yth[...], ytl[...])
            return 0

        lax.fori_loop(0, rows // tile, body, 0)

    def blocks(d):
        lax.fori_loop(0, 2, lambda i, _: (block(at(d * (1 - 2 * i))), 0)[1], 0)

    for s in range(1, nr):
        ag_wait(s - 1)
        if s < nr - 1:
            ag_send(s)
        if s == nr // 2:
            peers_wait(nc, col, x_s, x_r, lambda k: x_full.at[k], in_col)
            lax.fori_loop(0, nc, prep_x, 0)
            lax.fori_loop(0, 2, lambda i, _: (block(at(i * s)), 0)[1], 0)
        elif s > nr // 2:
            blocks(s)

    rt = 32

    def row_pass(ph, keep):
        def body(i, _):
            r0 = pl.ds(pl.multiple_of(i * rt, rt), rt)
            top = scores[r0, 0:128] + gvec[:, 0:128]
            for c in range(128, cols, 128):
                top = jnp.maximum(top, scores[r0, c:c + 128] + gvec[:, c:c + 128])
            top = jnp.broadcast_to(jnp.max(top, axis=1, keepdims=True), (rt, 128))
            acc = jnp.zeros((rt, 128), jnp.float32)
            for c in range(0, cols, 128):
                e = jnp.exp2(scores[r0, c:c + 128] + gvec[:, c:c + 128] - top)
                acc = acc + e
                if keep:
                    eh[r0, c:c + 128], el[r0, c:c + 128] = split(e)
            pm[r0, :] = top
            ps[r0, :] = acc
            return 0

        lax.fori_loop(0, rows // rt, body, 0, unroll=2)
        rstat[ph, col, 0:1, :] = jnp.max(pm[...].T, axis=0, keepdims=True)
        rstat[ph, col, 1:2, :] = jnp.sum(ps[...].T, axis=0, keepdims=True)
        peers(nc, col, rst_s.at[ph], rst_r.at[ph], rstat.at[ph, col], rstat.at[ph, col], in_col)

    def merge(ref, n):
        peak = ref[0, 0:1, :]
        for k in range(1, n):
            peak = jnp.maximum(peak, ref[k, 0:1, :])
        total = ref[0, 1:2, :] * jnp.exp2(ref[0, 0:1, :] - peak)
        for k in range(1, n):
            total = total + ref[k, 1:2, :] * jnp.exp2(ref[k, 0:1, :] - peak)
        return peak, total

    def row_merge(ph):
        peers_wait(nc, col, rst_s.at[ph], rst_r.at[ph], lambda k: rstat.at[ph, k], in_col)
        return merge(rstat.at[ph], nc)

    def to_column(v):
        fcol[...] = jnp.broadcast_to(v, (128, rows)).T

    def col_pass(ph, keep):
        def body(i, _):
            c0 = pl.ds(pl.multiple_of(i * 128, 128), 128)
            a = scores[:, c0] + fcol[...]
            top = jnp.max(a, axis=0, keepdims=True)
            e = jnp.exp2(a - top)
            cstat[ph, row, 0:1, c0] = top
            cstat[ph, row, 1:2, c0] = jnp.sum(e, axis=0, keepdims=True)
            if keep:
                eh[:, c0], el[:, c0] = split(e)
            return 0

        lax.fori_loop(0, cols // 128, body, 0)
        peers(nr, row, cst_s.at[ph], cst_r.at[ph], cstat.at[ph, row], cstat.at[ph, row], in_row)

    def col_merge(ph):
        peers_wait(nr, row, cst_s.at[ph], cst_r.at[ph], lambda k: cstat.at[ph, k], in_row)
        return merge(cstat.at[ph], nr)

    gvec[...] = yn[...] * -UNIT
    for it in range(2):
        row_pass(it, False)
        peak, total = row_merge(it)
        f_new = -(peak + jnp.log2(total))
        if it == 1:
            f_ref[...] = f_new * BACK + xn[...]
        to_column(f_new)
        col_pass(it, it == 1)
        if it == 0:
            peak, total = col_merge(0)
            gvec[...] = -(peak + jnp.log2(total))

    def chunk(o):
        return pl.ds(pl.multiple_of(o * yb, yb), yb)

    def weigh(s, d):
        c0 = chunk(at(-sides[d] * (1 + s)))
        w0 = pl.ds(d * hw, hw)
        part[w0, c0] = dot3(xth[w0, :], xtl[w0, :], eh[:, c0], el[:, c0])

    def weigh_steps(lo, hi):
        def body(s, _):
            for d in range(2):
                weigh(s, d)
            return 0

        lax.fori_loop(lo, hi, body, 0)

    def mine(s, d):
        c0 = chunk(at(-sides[d] * (1 + s)))
        return part[pl.ds(d * hw, hw), c0] * cloc[:, c0]

    def rs_step(s):
        for d in range(2):
            if s == 0:
                first[d] = mine(0, d)
                src = first.at[d]
            else:
                src = rsbuf.at[s - 1, d]
                arrive(src, rs_s.at[s - 1, d], rs_r.at[s - 1, d], (at(sides[d]), col))
                rsbuf[s - 1, d] = rsbuf[s - 1, d] + mine(s, d)
            if s < nr - 1:
                send(src, rsbuf.at[s, d], rs_s.at[s, d], rs_r.at[s, d], (at(sides[d]), col))

    weigh_steps(0, nr // 2)
    peak, total = col_merge(1)
    cloc[...] = jnp.exp2(cstat[1, row, 0:1, :] - peak) / total * (1.0 / SCALE)
    rs_step(0)
    gvec[...] = -(peak + jnp.log2(total))
    g_ref[...] = gvec[...] * BACK + yn[...]
    weigh_steps(nr // 2, nr)
    rs_step(1)

    row_pass(2, True)
    rs_step(2)

    def spread(k):
        r0 = pl.ds(pl.multiple_of(k * xb, xb), xb)
        npart[r0, :] = dot3(eh[r0, :], el[r0, :], ysh[...], ysl[...])

    mid = max(1, nc // 2)
    lax.fori_loop(0, mid, lambda i, _: (spread(lax.rem(col + 1 + i, nc)), 0)[1], 0)
    peak, total = row_merge(2)
    to_column(jnp.exp2(rstat[2, col, 0:1, :] - peak) / total)

    def scaled(k):
        r0 = pl.ds(pl.multiple_of(k * xb, xb), xb)
        fc = fcol[r0, :]
        for c in range(0, w, 128):
            npart[r0, c:c + 128] = npart[r0, c:c + 128] * fc
        return r0

    def push(o):
        k = lax.rem(col + o, nc)
        r0 = scaled(k)
        send(npart.at[r0], nsbuf.at[col], ns_s.at[o], ns_r.at[col], in_col(k))

    for o in range(1, min(mid + 1, nc)):
        push(o)
    if nr > 4:
        rs_step(3)
    lax.fori_loop(mid, nc, lambda i, _: (spread(lax.rem(col + 1 + i, nc)), 0)[1], 0)
    for o in range(mid + 1, nc):
        push(o)
    nsbuf[col] = npart[scaled(col), :]
    for s in range(4 if nr > 4 else 3, nr):
        rs_step(s)
    for d in range(2):
        dt_ref[:, d * hw:(d + 1) * hw] = rsbuf[nr - 2, d].T
    peers_wait(nc, col, ns_s, ns_r, lambda k: nsbuf.at[k], in_col)
    acc = nsbuf[0]
    for k in range(1, nc):
        acc = acc + nsbuf[k]
    nt_ref[...] = acc
    for c in pending:
        c.wait_send()


def solution(mesh):
    nr, nc = mesh.shape["row"], mesh.shape["col"]

    def shards(noise, data):
        xb, w = noise.shape
        yb = data.shape[0]
        rows, cols = xb * nc, yb * nr
        f32, bf = jnp.float32, jnp.bfloat16
        vmem = pltpu.VMEM
        dma = pltpu.SemaphoreType.DMA
        out = pl.pallas_call(
            functools.partial(kernel, nr, nc),
            out_shape=(
                jax.ShapeDtypeStruct((xb, w), f32),
                jax.ShapeDtypeStruct((yb, w), f32),
                jax.ShapeDtypeStruct((1, rows), f32),
                jax.ShapeDtypeStruct((1, cols), f32),
            ),
            in_specs=[pl.BlockSpec(memory_space=pltpu.VMEM)] * 2,
            out_specs=(pl.BlockSpec(memory_space=pltpu.VMEM),) * 4,
            scratch_shapes=[
                vmem((nc, xb, w), f32), vmem((nr, yb, w), f32), vmem((rows, cols), f32),
                vmem((rows, w), bf), vmem((rows, w), bf), vmem((w, rows), bf), vmem((w, rows), bf),
                vmem((cols, w), bf), vmem((cols, w), bf), vmem((w, yb), bf), vmem((w, yb), bf),
                vmem((rows, cols), bf), vmem((rows, cols), bf), vmem((w, cols), f32), vmem((rows, w), f32),
                vmem((rows, 128), f32), vmem((rows, 128), f32), vmem((rows, 128), f32),
                vmem((1, rows), f32), vmem((1, cols), f32), vmem((1, cols), f32), vmem((1, cols), f32),
                vmem((3, nc, 2, rows), f32), vmem((2, nr, 2, cols), f32),
                vmem((nr - 1, 2, w // 2, yb), f32), vmem((2, w // 2, yb), f32), vmem((nc, xb, w), f32),
                dma((nr - 1, 2)), dma((nr - 1, 2)), dma((nc,)), dma((nc,)),
                dma((3, nc)), dma((3, nc)), dma((2, nr)), dma((2, nr)),
                dma((nr - 1, 2)), dma((nr - 1, 2)), dma((nc,)), dma((nc,)),
            ],
            compiler_params=pltpu.CompilerParams(
                collective_id=0, has_side_effects=True, vmem_limit_bytes=60 * 1024 * 1024
            ),
        )(noise, data)
        return out[0], out[1], out[2].reshape(rows), out[3].reshape(cols)

    return jax.shard_map(
        shards,
        mesh=mesh,
        in_specs=(P(("row", "col"), None), P(("col", "row"), None)),
        out_specs=(P(("row", "col"), None), P(("col", "row"), None), P("row"), P("col")),
        check_vma=False,
    )
```

time: 432 us -> 145 us (0.34)
  waiting for transfers between devices: 203 us -> 0 us
  Pallas kernels: 0 us -> 139 us
  blocking collectives: 110 us -> 0 us
  matrix products: 59.7 us -> 0 us
  other arithmetic: 43.9 us -> 0 us
  between operations: 13.9 us -> 0.65 us
    pallas_call x0 -> x1, Pallas kernels: none -> 139 us  [shards(): pl.pallas_call(functools.partial(kernel, nr, nc), out_shape=(jax.ShapeDty...]
    reduce_scatter x2 -> x0, waiting for transfers between devices: 103 us -> none  [the longest x1 92.4 us: shards(): lax.psum_scatter(data_part, 'row', scatter_dimension=0, tiled=True)]
    all_gather x2 -> x0, waiting for transfers between devices: 99.3 us -> none  [the longest x1 73.1 us: shards(): y_full = lax.all_gather(data, 'row', axis=0, tiled=True)]
    dot_general x3 -> x0, matrix products: 59.7 us -> none  [the longest x1 22.4 us: shards(): jnp.dot(weights, y_full, precision=lax.Precision.HIGHEST, preferred_eleme...]
    pmax x5 -> x0, blocking collectives: 55.3 us -> none  [the longest x2 38.4 us: col_stats(): peak = lax.pmax(jnp.max(scores, axis=0), 'row')]
    psum x5 -> x0, blocking collectives: 54.8 us -> none  [the longest x2 35.4 us: col_stats(): total = lax.psum(jnp.sum(jnp.exp(scores - peak[None, :]), axis=0), 'row')]
    reduce_sum x7 -> x0, other arithmetic: 26.8 us -> none  [the longest x3 13.5 us: row_stats(): total = lax.psum(jnp.sum(jnp.exp(scores - peak[:, None]), axis=1), 'col')]
    reduce_max x4 -> x0, other arithmetic: 17.1 us -> none  [the longest x2 8.55 us: col_stats(): peak = lax.pmax(jnp.max(scores, axis=0), 'row')]
  transfers between devices with their start and end apart: 4 -> 0, of which waited for: 4 -> 0; matrix products, arithmetic and copies ran while one was open for 5% -> 0% of each run, Pallas kernels for 0% -> 0%
where the time goes in v1:
time: 145 us; the launch traced here: 144 us
  Pallas kernels  139 us (96%)
  local copies, waits for them, and re-layouts  4.03 us (3%)
    pallas_call x1, Pallas kernels, shards(): pl.pallas_call(functools.partial(kernel, nr, nc), out_shape=(jax.ShapeDty...  139 us
    unnamed x10, local copies, waits for them, and re-layouts  4.03 us

profile of v1, /device:TPU:0, one launch (start us, length us, event | category | flops | bytes accessed | tf_op | source)
XLA Modules:
  0.0 144.0 jit_solution(4273908720585255031)
XLA Ops:
  0.6 139.4 %shard_map.57 = (f32[256,512]{1,0:T(8,128)}, f32[256,512]{1,0:T(8,128)}, f32[1,1024]{1,0:T(1,128)}, f32[1,2048]{1,0:T(1,128)}) custom-call(f32[256,512]{1,0:T(8,128)} %x_ref.1, f32[256,512]{1,0:T(8,128)} %y_ref.1), custom_call_target="tpu_custom_call" | custom-call | tf_op jit(solution)/shard_map/pallas_call | solution.py:310
  140.0 0.0 copy-start
  140.0 1.9 %copy.10 = f32[256,512]{1,0:T(8,128)} copy(f32[256,512]{1,0:T(8,128)} %get-tuple-element.16) | data formatting | bytes 1048576
  141.9 0.0 copy-done
  141.9 0.0 copy-start.2
  141.9 0.8 copy.11
  142.7 0.0 copy-done.2
  142.7 0.0 copy-start.1
  142.7 0.6 copy.12
  143.3 0.1 copy-done.1
  143.4 0.6 copy.13
Async XLA Ops:
  140.0 1.9 %copy-start = (f32[256,512]{1,0:T(8,128)S(1)}, f32[256,512]{1,0:T(8,128)}, u32[]{:S(2)}) copy-start(f32[256,512]{1,0:T(8,128)} %get-tuple-element.17) | copy-start | bytes 1572868
  141.9 0.8 copy-start.2
  142.7 0.7 copy-start.1

commit v2 on v1

--- a/solution.py
+++ b/solution.py
@@ -13,6 +13,8 @@
 UNIT = math.log2(math.e) / EPSILON
 BACK = EPSILON * math.log(2.0)
 SCALE = 2.0 * UNIT
+PIECES = 2
+LOWEST = -3e38
 
 
 def split(v):
@@ -39,6 +41,7 @@
     yb = y_ref.shape[0]
     rows, cols = scores.shape
     half, hw = yb // 2, w // 2
+    hy, hq = half // PIECES, hw // PIECES
 
     def index_of(p):
         q = lax.div(p, nr // 2)
@@ -68,19 +71,19 @@
     def arrive(dst, ss, rs, dev):
         pltpu.make_async_remote_copy(src_ref=dst, dst_ref=dst, send_sem=ss, recv_sem=rs, device_id=dev, device_id_type=MESH).wait_recv()
 
-    def piece(ref, o, d):
-        return ref.at[o, pl.ds(d * half, half)]
-
-    def ag_send(s):
-        for d in range(2):
-            o = at(-sides[d] * s)
-            src = y_ref.at[pl.ds(d * half, half)] if s == 0 else piece(y_full, o, d)
-            send(src, piece(y_full, o, d), ag_s.at[s, d], ag_r.at[s, d], (at(sides[d]), col))
-
-    def ag_wait(s):
-        for d in range(2):
-            o = at(-sides[d] * (s + 1))
-            arrive(piece(y_full, o, d), ag_s.at[s, d], ag_r.at[s, d], (at(sides[d]), col))
+    def piece(ref, o, d, q):
+        return ref.at[o, pl.ds(d * half + q * hy, hy)]
+
+    def ag_step(s):
+        for q in range(PIECES):
+            for d in range(2):
+                o, dev = at(-sides[d] * s), (at(sides[d]), col)
+                dst = piece(y_full, o, d, q)
+                if s > 0:
+                    arrive(dst, ag_s.at[s - 1, d, q], ag_r.at[s - 1, d, q], dev)
+                if s < nr - 1:
+                    src = y_ref.at[pl.ds(d * half + q * hy, hy)] if s == 0 else dst
+                    send(src, dst, ag_s.at[s, d, q], ag_r.at[s, d, q], dev)
 
     def peers(n, me, ss, rs, src, dst, dev):
         for o in range(1, n):
@@ -94,9 +97,11 @@
     in_col = lambda k: (row, k)
     in_row = lambda k: (k, col)
 
-    ag_send(0)
+    ag_step(0)
     peers(nc, col, x_s, x_r, x_ref, x_full.at[col], in_col)
     x_full[col] = x_ref[...]
+    pm[...] = jnp.full_like(pm, LOWEST)
+    ps[...] = jnp.zeros_like(ps)
     y_full[row] = y_ref[...]
 
     def prep_x(k, _):
@@ -116,11 +121,24 @@
         ysh[c0, :], ysl[c0, :] = split(v)
         t = v.T
         yth[...], ytl[...] = split(t)
-        yn[:, c0] = jnp.sum(t * t, axis=0, keepdims=True)
+        norm = jnp.sum(t * t, axis=0, keepdims=True)
+        yn[:, c0] = norm
+        start = norm * -UNIT
 
         def body(i, _):
             r0 = pl.ds(pl.multiple_of(i * tile, tile), tile)
-            scores[r0, c0] = dot3(xsh[r0, :], xsl[r0, :], yth[...], ytl[...])
+            v = dot3(xsh[r0, :], xsl[r0, :], yth[...], ytl[...])
+            scores[r0, c0] = v
+            v = v + start
+            old = pm[r0, :]
+            top = old
+            for c in range(0, yb, 128):
+                top = jnp.maximum(top, v[:, c:c + 128])
+            acc = ps[r0, :] * jnp.exp2(old - top)
+            for c in range(0, yb, 128):
+                acc = acc + jnp.exp2(v[:, c:c + 128] - top)
+            pm[r0, :] = top
+            ps[r0, :] = acc
             return 0
 
         lax.fori_loop(0, rows // tile, body, 0)
@@ -129,9 +147,7 @@
         lax.fori_loop(0, 2, lambda i, _: (block(at(d * (1 - 2 * i))), 0)[1], 0)
 
     for s in range(1, nr):
-        ag_wait(s - 1)
-        if s < nr - 1:
-            ag_send(s)
+        ag_step(s)
         if s == nr // 2:
             peers_wait(nc, col, x_s, x_r, lambda k: x_full.at[k], in_col)
             lax.fori_loop(0, nc, prep_x, 0)
@@ -159,8 +175,13 @@
             return 0
 
         lax.fori_loop(0, rows // rt, body, 0, unroll=2)
-        rstat[ph, col, 0:1, :] = jnp.max(pm[...].T, axis=0, keepdims=True)
-        rstat[ph, col, 1:2, :] = jnp.sum(ps[...].T, axis=0, keepdims=True)
+        row_send(ph)
+
+    def row_send(ph):
+        tops = pm[...].T
+        top = jnp.max(tops, axis=0, keepdims=True)
+        rstat[ph, col, 0:1, :] = top
+        rstat[ph, col, 1:2, :] = jnp.sum(ps[...].T * jnp.exp2(tops - top), axis=0, keepdims=True)
         peers(nc, col, rst_s.at[ph], rst_r.at[ph], rstat.at[ph, col], rstat.at[ph, col], in_col)
 
     def merge(ref, n):
@@ -198,9 +219,11 @@
         peers_wait(nr, row, cst_s.at[ph], cst_r.at[ph], lambda k: cstat.at[ph, k], in_row)
         return merge(cstat.at[ph], nr)
 
-    gvec[...] = yn[...] * -UNIT
     for it in range(2):
-        row_pass(it, False)
+        if it == 0:
+            row_send(it)
+        else:
+            row_pass(it, False)
         peak, total = row_merge(it)
         f_new = -(peak + jnp.log2(total))
         if it == 1:
@@ -227,21 +250,26 @@
 
         lax.fori_loop(lo, hi, body, 0)
 
-    def mine(s, d):
-        c0 = chunk(at(-sides[d] * (1 + s)))
-        return part[pl.ds(d * hw, hw), c0] * cloc[:, c0]
-
     def rs_step(s):
-        for d in range(2):
-            if s == 0:
-                first[d] = mine(0, d)
-                src = first.at[d]
-            else:
-                src = rsbuf.at[s - 1, d]
-                arrive(src, rs_s.at[s - 1, d], rs_r.at[s - 1, d], (at(sides[d]), col))
-                rsbuf[s - 1, d] = rsbuf[s - 1, d] + mine(s, d)
-            if s < nr - 1:
-                send(src, rsbuf.at[s, d], rs_s.at[s, d], rs_r.at[s, d], (at(sides[d]), col))
+        for q in range(PIECES):
+            for d in range(2):
+                c0 = chunk(at(-sides[d] * (1 + s)))
+                own = part[pl.ds(d * hw + q * hq, hq), c0] * cloc[:, c0]
+                cut, dev = pl.ds(q * hq, hq), (at(sides[d]), col)
+                if s == 0:
+                    src = first.at[d, cut]
+                    first[d, cut] = own
+                else:
+                    src = rsbuf.at[s - 1, d, cut]
+                    arrive(src, rs_s.at[s - 1, d, q], rs_r.at[s - 1, d, q], dev)
+                    own = rsbuf[s - 1, d, cut] + own
+                    if s < nr - 1:
+                        rsbuf[s - 1, d, cut] = own
+                if s < nr - 1:
+                    send(src, rsbuf.at[s, d, cut], rs_s.at[s, d, q], rs_r.at[s, d, q], dev)
+                else:
+                    w0 = d * hw + q * hq
+                    dt_ref[:, w0:w0 + hq] = own.T
 
     weigh_steps(0, nr // 2)
     peak, total = col_merge(1)
@@ -284,15 +312,14 @@
     for o in range(mid + 1, nc):
         push(o)
     nsbuf[col] = npart[scaled(col), :]
-    for s in range(4 if nr > 4 else 3, nr):
+    for s in range(4 if nr > 4 else 3, nr - 1):
         rs_step(s)
-    for d in range(2):
-        dt_ref[:, d * hw:(d + 1) * hw] = rsbuf[nr - 2, d].T
     peers_wait(nc, col, ns_s, ns_r, lambda k: nsbuf.at[k], in_col)
     acc = nsbuf[0]
     for k in range(1, nc):
         acc = acc + nsbuf[k]
     nt_ref[...] = acc
+    rs_step(nr - 1)
     for c in pending:
         c.wait_send()
 
@@ -326,9 +353,9 @@
                 vmem((1, rows), f32), vmem((1, cols), f32), vmem((1, cols), f32), vmem((1, cols), f32),
                 vmem((3, nc, 2, rows), f32), vmem((2, nr, 2, cols), f32),
                 vmem((nr - 1, 2, w // 2, yb), f32), vmem((2, w // 2, yb), f32), vmem((nc, xb, w), f32),
-                dma((nr - 1, 2)), dma((nr - 1, 2)), dma((nc,)), dma((nc,)),
+                dma((nr - 1, 2, PIECES)), dma((nr - 1, 2, PIECES)), dma((nc,)), dma((nc,)),
                 dma((3, nc)), dma((3, nc)), dma((2, nr)), dma((2, nr)),
-                dma((nr - 1, 2)), dma((nr - 1, 2)), dma((nc,)), dma((nc,)),
+                dma((nr - 1, 2, PIECES)), dma((nr - 1, 2, PIECES)), dma((nc,)), dma((nc,)),
             ],
             compiler_params=pltpu.CompilerParams(
                 collective_id=0, has_side_effects=True, vmem_limit_bytes=60 * 1024 * 1024

time: 145 us -> 132 us (0.910)
  Pallas kernels: 139 us -> 127 us
    pallas_call x1, Pallas kernels: 139 us -> 127 us  [shards(): pl.pallas_call(functools.partial(kernel, nr, nc), out_shape=(jax.ShapeDty...]
where the time goes in v2:
time: 132 us; the launch traced here: 131 us
  Pallas kernels  127 us (96%)
  local copies, waits for them, and re-layouts  4.03 us (3%)
    pallas_call x1, Pallas kernels, shards(): pl.pallas_call(functools.partial(kernel, nr, nc), out_shape=(jax.ShapeDty...  127 us
    unnamed x10, local copies, waits for them, and re-layouts  4.03 us

profile of v2, /device:TPU:0, one launch (start us, length us, event | category | flops | bytes accessed | tf_op | source)
XLA Modules:
  0.0 131.3 jit_solution(9886658136693337617)
XLA Ops:
  0.6 126.7 %shard_map.57 = (f32[256,512]{1,0:T(8,128)}, f32[256,512]{1,0:T(8,128)}, f32[1,1024]{1,0:T(1,128)}, f32[1,2048]{1,0:T(1,128)}) custom-call(f32[256,512]{1,0:T(8,128)} %x_ref.1, f32[256,512]{1,0:T(8,128)} %y_ref.1), custom_call_target="tpu_custom_call" | custom-call | tf_op jit(solution)/shard_map/pallas_call | solution.py:337
  127.3 0.0 copy-start
  127.3 1.9 %copy.10 = f32[256,512]{1,0:T(8,128)} copy(f32[256,512]{1,0:T(8,128)} %get-tuple-element.16) | data formatting | bytes 1048576
  129.2 0.0 copy-done
  129.2 0.0 copy-start.2
  129.2 0.8 copy.11
  130.0 0.0 copy-done.2
  130.0 0.0 copy-start.1
  130.0 0.6 copy.12
  130.6 0.1 copy-done.1
  130.7 0.6 copy.13
Async XLA Ops:
  127.3 1.9 %copy-start = (f32[256,512]{1,0:T(8,128)S(1)}, f32[256,512]{1,0:T(8,128)}, u32[]{:S(2)}) copy-start(f32[256,512]{1,0:T(8,128)} %get-tuple-element.17) | copy-start | bytes 1572868
  129.2 0.8 copy-start.2
  130.0 0.7 copy-start.1
